TPU v7x, 32 devices: a whole 2x2x4 slice. The times are simulated.
32 devices in a mesh: grp: 8 (over y, x, core), seq: 4 (over z).
Axes of the slice: x: 2, y: 2, z: 4, core: 2. Of those that a mesh axis runs over, the one named last changes fastest.
Arguments:
- features: bfloat16 [8, 32, 64, 512], P('grp', 'seq'), may hold values from -6 to 6
- gn_gain: float32 [512], replicated, may hold values from 0.25 to 1.75
- gn_bias: float32 [512], replicated, may hold values from -3 to 3
- conv_weight: bfloat16 [8, 9, 512], replicated, may hold values from -0.09375 to 0.09375
- conv_bias: float32 [8], replicated, may hold values from -3 to 3
- quant_weight: float32 [4, 8], replicated, may hold values from -3 to 3
- quant_bias: float32 [4], replicated, may hold values from -3 to 3
- route: int32 [8], replicated, may hold values from 0 to 7, as said below
- bucket: int32 [8, 2], replicated, may hold values from 8 to 32, as said below
- times: float32 [8], P('grp'), may hold values from 0.05 to 0.95
- noise: float32 [8, 8192], P('grp'), may hold values from -6 to 6
- modulation: float32 [8, 2, 3072], P('grp'), may hold values from -3 to 3
- embed_weight: bfloat16 [16, 3072], replicated, may hold values from -1.5 to 1.5
- qkv_weight: bfloat16 [3072, 3, 512], P(None, None, 'seq'), may hold values from -1 to 1
Outputs:
- attended: bfloat16 [8, 512, 512], P('grp', 'seq')
Inputs may be any that keep to these rules, and one draw needn't show every extreme that they name: `bucket`: column 0 is an image's height (at most 16, at least half of it) and column 1 its width (at most 32, at least half of it); some image fills both. `route`: each trainer group receives exactly one image; some image g goes to group (g + 4) mod 8.
All inputs are finite; a program needn't handle non-finite values.
Results may differ from a plain program's by a relative error of at most 0.011.
Values may be sent and summed in bfloat16 or wider, within the bound.
A program may use at most 128 MiB of HBM per device.

v0:
```python
import functools

import numpy as np
import jax
import jax.numpy as jnp
from jax import lax
from jax.experimental import pallas as pl
from jax.experimental.pallas import tpu as pltpu
from jax.sharding import PartitionSpec as P

HEAD = 128
GROUPS = 32
PATCH = 16
EPS = 1e-06
MESH = pl.DeviceIdType.MESH
F32 = jnp.float32
BF16 = jnp.bfloat16
HIGHEST = lax.Precision.HIGHEST


def iota(shape, dim):
    return lax.broadcasted_iota(jnp.int32, shape, dim)


def one(cond, dtype=F32):
    return jnp.where(cond, 1.0, 0.0).astype(dtype)


def split2(x):
    hi = x.astype(BF16)
    return hi, (x - hi.astype(F32)).astype(BF16)


def split3(x):
    hi = x.astype(BF16)
    rest = x - hi.astype(F32)
    mid, low = split2(rest)
    return hi, mid, low


def mm(a, b, precision=None):
    return jnp.dot(a, b, preferred_element_type=F32, precision=precision)


def mm_nt(a, b):
    return lax.dot_general(a, b, (((1,), (1,)), ((), ())), preferred_element_type=F32)


def select3(x, chosen):
    hi, mid, low = split3(x)
    return mm(hi, chosen) + mm(mid, chosen) + mm(low, chosen)


def position_rows(rows, cols, width):
    quarter = width // 4
    freq = (np.float32(10000.0) ** (-np.arange(quarter, dtype=np.float32) / np.float32(quarter))).astype(np.float32)
    table = np.zeros((rows + cols, width), np.float64)
    for start, count, base in ((0, rows, 0), (rows, cols, 2 * quarter)):
        angle = (np.arange(count, dtype=np.float32)[:, None] * freq[None, :]).astype(np.float64)
        table[start : start + count, base : base + quarter] = np.sin(angle)
        table[start : start + count, base + quarter : base + 2 * quarter] = np.cos(angle)
    table = table - table.mean(axis=1, keepdims=True)
    return table.astype(np.float32)


def kernel(
    n,
    g,
    dims,
    route_ref,
    bucket_ref,
    times_ref,
    feat_hbm,
    w_hbm,
    table_hbm,
    gain_ref,
    gbias_ref,
    conv_ref,
    cbias_ref,
    quant_ref,
    qbias_ref,
    noise_ref,
    mod_ref,
    embed_ref,
    out_ref,
    feat,
    w_ref,
    table,
    xperm,
    stats,
    lat,
    gath,
    bw_all,
    bwt,
    bc,
    bs,
    at,
    pick,
    local_sem,
    st_send,
    st_recv,
    lat_send,
    lat_recv,
    ga_send,
    ga_recv,
    bw_send,
    bw_recv,
):
    strip_rows, lat_cols, chans, seq_tokens, width = dims
    cells = strip_rows * lat_cols
    plane = cells // 4
    half = lat_cols // 2
    prow = strip_rows // 2
    patch_rows = prow * n
    kr = PATCH + patch_rows + half
    kb = kr + 16
    per_group = chans // GROUPS
    me = lax.axis_index("seq")
    t = lax.axis_index("grp")

    load_feat = pltpu.make_async_copy(feat_hbm, feat, local_sem.at[0])
    load_table = pltpu.make_async_copy(table_hbm, table, local_sem.at[1])
    load_w = pltpu.make_async_copy(w_hbm, w_ref, local_sem.at[2])
    load_feat.start()
    load_table.start()
    load_w.start()

    barrier = pltpu.get_barrier_semaphore()
    for o in range(1, n):
        pl.semaphore_signal(barrier, inc=1, device_id={"seq": lax.rem(me + o, n)}, device_id_type=MESH)
    for o in range(1, g):
        pl.semaphore_signal(barrier, inc=1, device_id={"grp": lax.rem(t + o, g)}, device_id_type=MESH)

    def exchange(buf, send_sem, recv_sem, axis, mine, size):
        return [
            pltpu.make_async_remote_copy(
                src_ref=buf.at[mine],
                dst_ref=buf.at[mine],
                send_sem=send_sem.at[o],
                recv_sem=recv_sem.at[o],
                device_id={axis: lax.rem(mine + o, size)},
                device_id_type=MESH,
            )
            for o in range(1, size)
        ]

    ex_stats = exchange(stats, st_send, st_recv, "seq", me, n)
    ex_lat = exchange(lat, lat_send, lat_recv, "grp", t, g)
    ex_gath = exchange(gath, ga_send, ga_recv, "seq", me, n)
    ex_bw = exchange(bw_all, bw_send, bw_recv, "seq", me, n)

    height = bucket_ref[0, t]
    breadth = bucket_ref[1, t]
    cell = iota((cells, 1), 0)
    valid = ((cell // lat_cols + me * strip_rows) < 2 * height) & ((cell % lat_cols) < 2 * breadth)
    inside = one(valid)

    def inside_count(strip):
        rows = jnp.clip(2 * height - strip * strip_rows, 0, strip_rows)
        return (rows * 2 * breadth).astype(F32)

    load_feat.wait()
    x = feat[...].astype(F32)
    total = jnp.sum(x * inside, axis=0, keepdims=True)
    own = jnp.maximum(inside_count(me), 1.0)
    centred = (x - total / own) * inside
    second = jnp.sum(centred * centred, axis=0, keepdims=True)
    stats[me] = jnp.concatenate([total, second], axis=0)
    pl.semaphore_wait(barrier, n - 1 + g - 1)
    for copy in ex_stats:
        copy.start()

    order = iota((cells, cells), 0)
    ab, inner = order // plane, order % plane
    origin = (2 * (inner // half) + ab // 2) * lat_cols + 2 * (inner % half) + ab % 2
    perm = one(iota((cells, cells), 1) == origin, BF16)
    xperm[...] = mm(perm, feat[...]).astype(BF16)
    new = iota((cells, 1), 0)
    nab, ninner = new // plane, new % plane
    nrow = 2 * (ninner // half) + nab // 2 + me * strip_rows
    ncol = 2 * (ninner % half) + nab % 2
    inside_perm = one((nrow < 2 * height) & (ncol < 2 * breadth))
    same = one(iota((chans, chans), 0) // per_group == iota((chans, chans), 1) // per_group, BF16)

    load_table.wait()
    scale = 1.0 + mod_ref[1:2, :]
    shift = mod_ref[0:1, :]
    for i in range(kr // 16):
        if i == 0:
            block = embed_ref[...].astype(F32)
            block = block - jnp.mean(block, axis=1, keepdims=True)
        else:
            block = table[16 * (i - 1) : 16 * i, :]
        hi, low = split2(block)
        bc[16 * i : 16 * i + 16, :] = hi
        bc[kr + 16 * i : kr + 16 * i + 16, :] = low
        hi, low = split2(block * scale)
        bs[16 * i : 16 * i + 16, :] = hi
        bs[kb + 16 * i : kb + 16 * i + 16, :] = low
    hi, low = split2(jnp.where(iota((16, width), 0) == 0, shift, 0.0))
    bs[kr:kb, :] = hi
    bs[kb + kr : 2 * kb, :] = low
    load_w.wait()
    for i in range(3):
        both = mm(bs[...], w_ref[i])
        bw_all[me, :, i * HEAD : (i + 1) * HEAD] = (both[:kb] + both[kb:]).astype(BF16)
    for copy in ex_bw:
        copy.start()

    for copy in ex_stats:
        copy.wait_recv()
    pixels = (4 * height * breadth * per_group).astype(F32)
    sums = [stats[i] for i in range(n)]
    channel_sum = sums[0][0:1]
    for i in range(1, n):
        channel_sum = channel_sum + sums[i][0:1]
    eight = jnp.zeros((8, chans), F32)
    mean = select3(channel_sum + eight, same)[0:1] / pixels
    squares = jnp.zeros((1, chans), F32)
    for i in range(n):
        count = inside_count(i)
        away = sums[i][0:1] / jnp.maximum(count, 1.0) - mean
        squares = squares + sums[i][1:2] + count * away * away
    var = select3(squares + eight, same)[0:1] / pixels
    slope = lax.rsqrt(var + EPS) * gain_ref[...]
    y = (xperm[...].astype(F32) - mean) * slope + gbias_ref[...]
    y = y * (0.5 * jnp.tanh(0.5 * y) + 0.5) * inside_perm
    hidden = y.astype(BF16)

    taps = mm_nt(conv_ref[...], hidden)
    lane = iota((8, plane), 1)
    lane_q, lane_p = lane % half, lane // half

    def piece(dy, dx, a, b):
        k = 3 * dy + dx
        p = 2 * a + b
        return taps[8 * k : 8 * k + 8, p * plane : (p + 1) * plane]

    def across(dy, a, b):
        z = piece(dy, 1, a, b)
        if b == 0:
            prev = pltpu.roll(piece(dy, 0, a, 1), 1, axis=1)
            return z + jnp.where(lane_q == 0, 0.0, prev) + piece(dy, 2, a, 1)
        after = pltpu.roll(piece(dy, 2, a, 0), plane - 1, axis=1)
        return z + piece(dy, 0, a, 0) + jnp.where(lane_q == half - 1, 0.0, after)

    inner_planes, edge_planes = [], []
    for a in range(2):
        for b in range(2):
            z = across(1, a, b)
            if a == 0:
                moved = pltpu.roll(across(0, 1, b), half, axis=1)
                edge = lane_p == 0
                z = z + across(2, 1, b)
            else:
                moved = pltpu.roll(across(2, 0, b), plane - half, axis=1)
                edge = lane_p == prow - 1
                z = z + across(0, 0, b)
            inner_planes.append(z + jnp.where(edge, 0.0, moved))
            edge_planes.append(jnp.where(edge, moved, 0.0))
    stacked = jnp.concatenate(
        [jnp.concatenate(inner_planes, axis=0), jnp.concatenate(edge_planes, axis=0)], axis=1
    )
    pick_k = one(iota((PATCH, 4), 0) // 4 == iota((PATCH, 4), 1))
    quant_rows = mm(pick_k, quant_ref[...], HIGHEST)
    tile_o = one(iota((8, 32), 1) % 8 == iota((8, 32), 0))
    spread_q = mm(quant_rows, tile_o, HIGHEST)
    spread_q = jnp.where(iota((PATCH, 32), 0) % 4 == iota((PATCH, 32), 1) // 8, spread_q, 0.0)
    lat[t] = mm(spread_q, stacked, HIGHEST)
    for copy in ex_lat:
        copy.start()

    bias = jnp.sum(quant_rows * cbias_ref[...], axis=1, keepdims=True) + jnp.sum(
        pick_k * qbias_ref[...], axis=1, keepdims=True
    )
    source = jnp.int32(0)
    for i in range(g):
        source = jnp.where(route_ref[i] == t, i, source)
    tall = bucket_ref[0, source]
    wide = bucket_ref[1, source]
    alive_count = tall * wide
    token = iota((1, seq_tokens), 1)
    wide_f = jnp.full((1, seq_tokens), wide.astype(F32))
    row_f = jnp.floor((token.astype(F32) + 0.5) / wide_f)
    col_f = token.astype(F32) - row_f * wide_f
    row_i, col_i = row_f.astype(jnp.int32), col_f.astype(jnp.int32)
    alive = token < alive_count
    at[PATCH : PATCH + patch_rows, :] = one(iota((patch_rows, seq_tokens), 0) == row_i, BF16)
    at[PATCH + patch_rows : kr, :] = one(iota((half, seq_tokens), 0) == col_i, BF16)
    wanted = jnp.where(alive, row_i * half + col_i, -1)
    for i in range(n):
        pick[i * plane : (i + 1) * plane, :] = one(iota((plane, seq_tokens), 0) + i * plane == wanted, BF16)
    flat = noise_ref[...].T
    lines = seq_tokens * PATCH // 128
    noise_t = jnp.zeros((PATCH, seq_tokens), F32)
    where_line = iota((lines, seq_tokens), 0)
    where_token = iota((lines, seq_tokens), 1)
    for m in range(128 // PATCH):
        chosen = one(where_token == where_line * (128 // PATCH) + m, BF16)
        hi, low = split2(flat[PATCH * m : PATCH * m + PATCH, :])
        noise_t = noise_t + mm(hi, chosen) + mm(low, chosen)
    moment = times_ref[0]
    noise_t = noise_t * moment
    gram = mm_nt(bc[...], bc[...])
    gram = (gram[:kr, :kr] + gram[:kr, kr:] + gram[kr:, :kr] + gram[kr:, kr:]) * (1.0 / width)
    gram_hi, gram_low = split2(gram)

    for copy in ex_lat:
        copy.wait_recv()
    gath[me] = lat[source]
    for copy in ex_gath:
        copy.start()
    for copy in ex_bw:
        copy.wait_recv()
    for i in range(n):
        bwt[i] = bw_all[i].astype(F32).T.astype(BF16)
    for copy in ex_gath:
        copy.wait_recv()

    parts = [gath[i] for i in range(n)]
    upper = iota((PATCH, plane), 0) // 2 % 2 == 0
    pieces = []
    none = jnp.zeros((PATCH, plane), F32)
    for i in range(n):
        before = parts[i - 1][:, plane:] if i > 0 else none
        after = parts[i + 1][:, plane:] if i < n - 1 else none
        pieces.append(parts[i][:, :plane] + jnp.where(upper, before, after) + bias)
    patches = jnp.concatenate(pieces, axis=1)
    picked = select3(patches, pick[...])
    at[0:PATCH, :] = ((1.0 - moment) * picked + noise_t).astype(BF16)
    a_all = at[...]
    through = mm(gram_hi, a_all) + mm(gram_low, a_all)
    spread = jnp.sum(through * a_all.astype(F32), axis=0, keepdims=True)
    rstd = lax.rsqrt(jnp.maximum(spread, 0.0) + EPS)

    own_tokens = seq_tokens // n
    a_own = at[:, pl.ds(pl.multiple_of(me * own_tokens, own_tokens), own_tokens)]
    through_own = mm(gram_hi, a_own) + mm(gram_low, a_own)
    spread_own = jnp.sum(through_own * a_own.astype(F32), axis=0, keepdims=True)
    rstd_own = lax.rsqrt(jnp.maximum(spread_own, 0.0) + EPS)
    query_alive = (iota((own_tokens, 1), 0) + me * own_tokens) < alive_count
    for h in range(n):
        weights = bwt[h]
        biases = weights[:, kr : kr + 1].astype(F32)
        q_t = mm(weights[:HEAD, :kr], a_own) * rstd_own + biases[:HEAD]
        kv_t = mm(weights[HEAD:, :kr], a_all) * rstd + biases[HEAD:]
        kv_t = kv_t.astype(BF16)
        query = q_t.T.astype(BF16)
        scores = mm(query, kv_t[:HEAD]) * HEAD ** (-0.5)
        scores = jnp.where(alive, scores, -jnp.inf)
        powers = jnp.exp(scores - jnp.max(scores, axis=1, keepdims=True))
        probabilities = (powers * (1.0 / jnp.sum(powers, axis=1, keepdims=True))).astype(BF16)
        attended = mm_nt(probabilities, kv_t[HEAD:])
        out_ref[:, h * HEAD : (h + 1) * HEAD] = jnp.where(query_alive, attended, 0.0).astype(BF16)

    for copies in (ex_stats, ex_bw, ex_lat, ex_gath):
        for copy in copies:
            copy.wait_send()


def solution(mesh):
    n, g = mesh.shape["seq"], mesh.shape["grp"]

    def per_device(
        features,
        gn_gain,
        gn_bias,
        conv_weight,
        conv_bias,
        quant_weight,
        quant_bias,
        route,
        bucket,
        times,
        noise,
        modulation,
        embed_weight,
        qkv_weight,
    ):
        _, strip_rows, lat_cols, chans = features.shape
        width = embed_weight.shape[1]
        seq_tokens = noise.shape[1] // PATCH
        cells = strip_rows * lat_cols
        half = lat_cols // 2
        patch_rows = strip_rows // 2 * n
        plane = cells // 4
        kr = PATCH + patch_rows + half
        kb = kr + 16
        table = jnp.asarray(position_rows(patch_rows, half, width))
        dims = (strip_rows, lat_cols, chans, seq_tokens, width)
        vmem = pl.BlockSpec(memory_space=pltpu.VMEM)
        smem = pl.BlockSpec(memory_space=pltpu.SMEM)
        anywhere = pl.BlockSpec(memory_space=pl.ANY)
        dma = pltpu.SemaphoreType.DMA
        result = pl.pallas_call(
            functools.partial(kernel, n, g, dims),
            out_shape=jax.ShapeDtypeStruct((seq_tokens // n, n * HEAD), BF16),
            in_specs=[smem] * 3 + [anywhere] * 3 + [vmem] * 9,
            out_specs=vmem,
            scratch_shapes=[
                pltpu.VMEM((cells, chans), BF16),
                pltpu.VMEM((3, width, HEAD), BF16),
                pltpu.VMEM((patch_rows + half, width), F32),
                pltpu.VMEM((cells, chans), BF16),
                pltpu.VMEM((n, 2, chans), F32),
                pltpu.VMEM((g, PATCH, 2 * plane), F32),
                pltpu.VMEM((n, PATCH, 2 * plane), F32),
                pltpu.VMEM((n, kb, 3 * HEAD), BF16),
                pltpu.VMEM((n, 3 * HEAD, kb), BF16),
                pltpu.VMEM((2 * kr, width), BF16),
                pltpu.VMEM((2 * kb, width), BF16),
                pltpu.VMEM((kr, seq_tokens), BF16),
                pltpu.VMEM((n * plane, seq_tokens), BF16),
                dma((3,)),
                dma((n,)),
                dma((n,)),
                dma((g,)),
                dma((g,)),
                dma((n,)),
                dma((n,)),
                dma((n,)),
                dma((n,)),
            ],
            compiler_params=pltpu.CompilerParams(
                collective_id=0, has_side_effects=True, vmem_limit_bytes=56 << 20
            ),
        )(
            route,
            bucket.T,
            times,
            features.reshape(cells, chans),
            qkv_weight.transpose(1, 0, 2),
            table,
            gn_gain.reshape(1, chans),
            gn_bias.reshape(1, chans),
            conv_weight.transpose(1, 0, 2).reshape(-1, chans),
            conv_bias.reshape(1, -1),
            quant_weight,
            quant_bias.reshape(1, -1),
            noise.reshape(-1, 128),
            modulation[0],
            embed_weight,
        )
        return result[None]

    in_specs = (
        P("grp", "seq", None, None),
        P(),
        P(),
        P(),
        P(),
        P(),
        P(),
        P(),
        P(),
        P("grp"),
        P("grp", None),
        P("grp", None, None),
        P(),
        P(None, None, "seq"),
    )
    return jax.shard_map(
        per_device, mesh=mesh, in_specs=in_specs, out_specs=P("grp", "seq", None), check_vma=False
    )
```

profile of v0, /device:TPU:0, one launch (start us, length us, event | category | flops | bytes accessed | tf_op | source)
XLA Modules:
  0.0 25.4 jit_solution(12496950510303017576)
XLA Ops:
  0.7 23.2 %shard_map.145 = bf16[128,512]{1,0:T(8,128)(2,1)} custom-call(s32[8]{0:T(128)} %route_ref.1, s32[2,8]{1,0:T(2,128)} %bitcast.21, f32[1]{0:T(128)S(6)} %copy.17.times_ref, bf16[512,512]{1,0:T(8,128)(2,1)} %bitcast.15, bf16[3,3072,128]{2,1,0:T(8,128)(2,1)} %bitcast.13, f32[48,3072]{1,0:T(8,128)} %constant.2.clone.table_hbm, f32[1,512]{1,0:T(1,128)} %bitcast.19, ...), custom_call_target="tpu_custom_call" | custom-call | tf_op jit(solution)/shard_map/pallas_call | solution.py:395
  23.8 1.6 %copy.18 = bf16[1,128,512]{2,1,0:T(8,128)(2,1)} copy(bf16[1,128,512]{2,1,0:T(8,128)(2,1)} %bitcast.14) | data formatting | bytes 262144
where the time goes:
time: 25.6 us; the launch traced here: 25.4 us
  Pallas kernels  23.2 us (91%)
  local copies, waits for them, and re-layouts  1.57 us (6%)
  between operations  0.66 us (3%)
    pallas_call x1, Pallas kernels, per_device(): pl.pallas_call(functools.partial(kernel, n, g, dims), out_shape=jax.Shape...  23.2 us
    unnamed x1, local copies, waits for them, and re-layouts  1.57 us

commit v1 on v0

--- a/solution.py
+++ b/solution.py
@@ -67,12 +67,28 @@
     n,
     g,
     dims,
+    route_hbm,
+    bucket_hbm,
+    times_hbm,
+    feat_hbm,
+    w_hbm,
+    table_hbm,
+    gain_hbm,
+    gbias_hbm,
+    conv_hbm,
+    cbias_hbm,
+    quant_hbm,
+    qbias_hbm,
+    noise_hbm,
+    mod_hbm,
+    embed_hbm,
+    out_ref,
     route_ref,
     bucket_ref,
     times_ref,
-    feat_hbm,
-    w_hbm,
-    table_hbm,
+    feat,
+    w_ref,
+    table,
     gain_ref,
     gbias_ref,
     conv_ref,
@@ -82,10 +98,6 @@
     noise_ref,
     mod_ref,
     embed_ref,
-    out_ref,
-    feat,
-    w_ref,
-    table,
     xperm,
     stats,
     lat,
@@ -118,18 +130,26 @@
     me = lax.axis_index("seq")
     t = lax.axis_index("grp")
 
-    load_feat = pltpu.make_async_copy(feat_hbm, feat, local_sem.at[0])
-    load_table = pltpu.make_async_copy(table_hbm, table, local_sem.at[1])
-    load_w = pltpu.make_async_copy(w_hbm, w_ref, local_sem.at[2])
-    load_feat.start()
-    load_table.start()
-    load_w.start()
+    hbm = (
+        feat_hbm, bucket_hbm, route_hbm, times_hbm, table_hbm, embed_hbm, mod_hbm, w_hbm,
+        gain_hbm, gbias_hbm, conv_hbm, cbias_hbm, quant_hbm, qbias_hbm, noise_hbm,
+    )
+    local = (
+        feat, bucket_ref, route_ref, times_ref, table, embed_ref, mod_ref, w_ref,
+        gain_ref, gbias_ref, conv_ref, cbias_ref, quant_ref, qbias_ref, noise_ref,
+    )
+    loads = [pltpu.make_async_copy(a, b, local_sem.at[i]) for i, (a, b) in enumerate(zip(hbm, local))]
+    for copy in loads[:2]:
+        copy.start()
 
     barrier = pltpu.get_barrier_semaphore()
     for o in range(1, n):
         pl.semaphore_signal(barrier, inc=1, device_id={"seq": lax.rem(me + o, n)}, device_id_type=MESH)
     for o in range(1, g):
         pl.semaphore_signal(barrier, inc=1, device_id={"grp": lax.rem(t + o, g)}, device_id_type=MESH)
+
+    for copy in loads[2:]:
+        copy.start()
 
     def exchange(buf, send_sem, recv_sem, axis, mine, size):
         return [
@@ -149,6 +169,7 @@
     ex_gath = exchange(gath, ga_send, ga_recv, "seq", me, n)
     ex_bw = exchange(bw_all, bw_send, bw_recv, "seq", me, n)
 
+    loads[1].wait()
     height = bucket_ref[0, t]
     breadth = bucket_ref[1, t]
     cell = iota((cells, 1), 0)
@@ -159,7 +180,7 @@
         rows = jnp.clip(2 * height - strip * strip_rows, 0, strip_rows)
         return (rows * 2 * breadth).astype(F32)
 
-    load_feat.wait()
+    loads[0].wait()
     x = feat[...].astype(F32)
     total = jnp.sum(x * inside, axis=0, keepdims=True)
     own = jnp.maximum(inside_count(me), 1.0)
@@ -182,7 +203,8 @@
     inside_perm = one((nrow < 2 * height) & (ncol < 2 * breadth))
     same = one(iota((chans, chans), 0) // per_group == iota((chans, chans), 1) // per_group, BF16)
 
-    load_table.wait()
+    for copy in loads[4:7]:
+        copy.wait()
     scale = 1.0 + mod_ref[1:2, :]
     shift = mod_ref[0:1, :]
     for i in range(kr // 16):
@@ -200,13 +222,15 @@
     hi, low = split2(jnp.where(iota((16, width), 0) == 0, shift, 0.0))
     bs[kr:kb, :] = hi
     bs[kb + kr : 2 * kb, :] = low
-    load_w.wait()
+    loads[7].wait()
     for i in range(3):
         both = mm(bs[...], w_ref[i])
         bw_all[me, :, i * HEAD : (i + 1) * HEAD] = (both[:kb] + both[kb:]).astype(BF16)
     for copy in ex_bw:
         copy.start()
 
+    for copy in loads[2:4] + loads[8:]:
+        copy.wait()
     for copy in ex_stats:
         copy.wait_recv()
     pixels = (4 * height * breadth * per_group).astype(F32)
@@ -389,18 +413,29 @@
         table = jnp.asarray(position_rows(patch_rows, half, width))
         dims = (strip_rows, lat_cols, chans, seq_tokens, width)
         vmem = pl.BlockSpec(memory_space=pltpu.VMEM)
-        smem = pl.BlockSpec(memory_space=pltpu.SMEM)
         anywhere = pl.BlockSpec(memory_space=pl.ANY)
         dma = pltpu.SemaphoreType.DMA
         result = pl.pallas_call(
             functools.partial(kernel, n, g, dims),
-            out_shape=jax.ShapeDtypeStruct((seq_tokens // n, n * HEAD), BF16),
-            in_specs=[smem] * 3 + [anywhere] * 3 + [vmem] * 9,
+            out_shape=pltpu.VMEM((seq_tokens // n, n * HEAD), BF16),
+            in_specs=[anywhere] * 15,
             out_specs=vmem,
             scratch_shapes=[
+                pltpu.SMEM(route.shape, jnp.int32),
+                pltpu.SMEM(bucket.shape[::-1], jnp.int32),
+                pltpu.SMEM(times.shape, F32),
                 pltpu.VMEM((cells, chans), BF16),
                 pltpu.VMEM((3, width, HEAD), BF16),
                 pltpu.VMEM((patch_rows + half, width), F32),
+                pltpu.VMEM((1, chans), F32),
+                pltpu.VMEM((1, chans), F32),
+                pltpu.VMEM((9 * conv_weight.shape[0], chans), BF16),
+                pltpu.VMEM((1, conv_bias.shape[0]), F32),
+                pltpu.VMEM(quant_weight.shape, F32),
+                pltpu.VMEM((1, quant_bias.shape[0]), F32),
+                pltpu.VMEM((noise.shape[1] // 128, 128), F32),
+                pltpu.VMEM(modulation.shape[1:], F32),
+                pltpu.VMEM(embed_weight.shape, BF16),
                 pltpu.VMEM((cells, chans), BF16),
                 pltpu.VMEM((n, 2, chans), F32),
                 pltpu.VMEM((g, PATCH, 2 * plane), F32),
@@ -411,7 +446,7 @@
                 pltpu.VMEM((2 * kb, width), BF16),
                 pltpu.VMEM((kr, seq_tokens), BF16),
                 pltpu.VMEM((n * plane, seq_tokens), BF16),
-                dma((3,)),
+                dma((15,)),
                 dma((n,)),
                 dma((n,)),
                 dma((g,)),

time: 25.6 us -> 23.1 us (0.902)
  Pallas kernels: 23.2 us -> 21.6 us
  local copies, waits for them, and re-layouts: 1.57 us -> 0.66 us
    pallas_call x1, Pallas kernels: 23.2 us -> 21.6 us  [per_device(): pl.pallas_call(functools.partial(kernel, n, g, dims), out_shape=pltpu.VME...]
    unnamed x1, local copies, waits for them, and re-layouts: 1.57 us -> 0.66 us
where the time goes in v1:
time: 23.1 us; the launch traced here: 22.9 us
  Pallas kernels  21.6 us (94%)
  local copies, waits for them, and re-layouts  0.66 us (3%)
  between operations  0.66 us (3%)
    pallas_call x1, Pallas kernels, per_device(): pl.pallas_call(functools.partial(kernel, n, g, dims), out_shape=pltpu.VME...  21.6 us
    unnamed x1, local copies, waits for them, and re-layouts  0.66 us

profile of v1, /device:TPU:0, one launch (start us, length us, event | category | flops | bytes accessed | tf_op | source)
XLA Modules:
  0.0 22.9 jit_solution(9285671841819704913)
XLA Ops:
  0.7 21.6 %shard_map.145 = bf16[128,512]{1,0:T(8,128)(2,1)S(1)} custom-call(s32[8]{0:T(128)} %route_hbm.1, s32[2,8]{1,0:T(2,128)} %bitcast.21, f32[1]{0:T(128)S(6)} %copy.18.times_hbm, bf16[512,512]{1,0:T(8,128)(2,1)} %bitcast.15, bf16[3,3072,128]{2,1,0:T(8,128)(2,1)} %bitcast.14, f32[48,3072]{1,0:T(8,128)} %constant.2.clone.table_hbm, f32[1,512]{1,0:T(1,128)} %bitcast.19, ...), custom_call_target="tpu_custom_call" | custom-call | tf_op jit(solution)/shard_map/pallas_call | solution.py:418
  22.3 0.7 %copy.17 = bf16[1,128,512]{2,1,0:T(8,128)(2,1)} copy(bf16[1,128,512]{2,1,0:T(8,128)(2,1)S(1)} %bitcast.13) | data formatting | bytes 262144
